TPU v7x, 32 devices: a whole 2x2x4 slice. The times are simulated.
32 devices in a mesh: samp: 16 (over z, y, x), tgt: 2 (over core).
Axes of the slice: x: 2, y: 2, z: 4, core: 2. Of those that a mesh axis runs over, the one named last changes fastest.
Arguments:
- samples: bfloat16 [3072, 128], P('samp'), may hold values from -6 to 6
- omega: bfloat16 [128, 4096], replicated, may hold values from -0.5 to 0.5
- phase: float32 [4096], replicated, may hold values from -3.140625 to 3.140625
- right_side: float32 [4096, 512], P('samp', 'tgt'), may hold values from -6 to 6
Outputs:
- weights: float32 [4096, 512], P('samp', 'tgt')
All inputs are finite; a program needn't handle non-finite values.
Results may differ from a plain program's by a relative error of at most 0.011.
The roundings to bfloat16 on the way count: a program that leaves them out, or rounds other values in their place, can miss the bound.
Values may be sent and summed in bfloat16 or wider, within the bound.
A program may use at most 128 MiB of HBM per device.

v0:
```python
import math
import jax
import jax.numpy as jnp
from jax import lax
from jax.sharding import PartitionSpec as P

ITERS = 2
ridge = 1.0


def precise_dot(left_matrix, right_matrix):
    return jnp.dot(left_matrix, right_matrix, precision=lax.Precision.HIGHEST)


def spd_solve(gram_matrix, rhs_matrix):
    factor = jnp.linalg.cholesky(gram_matrix)
    return jax.scipy.linalg.cho_solve((factor, True), rhs_matrix)


def cosine_block(samples, omega, phase, first_row, row_count):
    omega_cols = lax.dynamic_slice_in_dim(omega, first_row, row_count, 1)
    phase_cols = lax.dynamic_slice_in_dim(phase, first_row, row_count, 0)
    preact = jnp.dot(samples, omega_cols, preferred_element_type=jnp.float32) + phase_cols
    return jnp.cos(preact).astype(jnp.bfloat16)


def full_gram(stacked):
    summed = lax.psum(stacked, "samp")
    return lax.all_gather(summed, "tgt", axis=2, tiled=True)


def body(samples, omega, phase, right_side):
    feat_rows, col_count = right_side.shape
    samp_count = lax.axis_size("samp")
    feat_total = omega.shape[1]
    sample_total = samples.shape[0] * samp_count
    col_offset = lax.axis_index("tgt") * col_count
    store_block = math.gcd(feat_total, 512)
    stored = jnp.concatenate(
        [
            cosine_block(samples, omega, phase, index_block * store_block, store_block)
            for index_block in range(feat_total // store_block)
        ],
        axis=1,
    )

    def columns(first_row, row_count):
        return lax.dynamic_slice_in_dim(stored, first_row, row_count, 1)

    resid_all = lax.all_gather(right_side, "tgt", axis=1, tiled=True)
    direction_all = resid_all
    weight_own = jnp.zeros_like(right_side)
    gram_rr = full_gram(precise_dot(resid_all.T, right_side)[None])[0]
    for iteration in range(ITERS):
        direction_own = lax.dynamic_slice_in_dim(direction_all, col_offset, col_count, 1)
        initial = jnp.zeros((samples.shape[0], col_count), jnp.float32)
        shard_piece = lax.all_gather(direction_own.astype(jnp.bfloat16), "samp", axis=0, tiled=True)
        piece_rows = shard_piece.shape[0]
        block_size = math.gcd(piece_rows, 512)

        def project_one_block(index_block, acc_value):
            begin_row = index_block * block_size
            sub_piece = lax.dynamic_slice_in_dim(shard_piece, begin_row, block_size, 0)
            return acc_value + jnp.dot(
                columns(begin_row, block_size), sub_piece, preferred_element_type=jnp.float32
            )

        projected = lax.fori_loop(0, piece_rows // block_size, project_one_block, initial)
        proj_bf = projected.astype(jnp.bfloat16)
        transpose_row_count = feat_rows * lax.axis_size("samp")
        transpose_block_size = math.gcd(transpose_row_count, 512)

        def transpose_one_block(index_block, result):
            begin_row = index_block * transpose_block_size
            feats_block = columns(begin_row, transpose_block_size)
            block_term = lax.dot_general(
                feats_block, proj_bf, (((0,), (0,)), ((), ())), preferred_element_type=jnp.float32
            )
            return lax.dynamic_update_slice_in_dim(result, block_term, begin_row, 0)

        zero_rows = jnp.zeros((transpose_row_count, col_count), jnp.float32)
        summed_image = lax.psum_scatter(
            lax.fori_loop(
                0, transpose_row_count // transpose_block_size, transpose_one_block, zero_rows
            ),
            "samp",
            scatter_dimension=0,
            tiled=True,
        )
        image_own = summed_image / sample_total + ridge * direction_own
        image_all = lax.all_gather(image_own, "tgt", axis=1, tiled=True)
        gram_pq = full_gram(precise_dot(direction_all.T, image_own)[None])[0]
        alpha_coef = spd_solve(gram_pq, gram_rr)
        alpha_own = lax.dynamic_slice_in_dim(alpha_coef, col_offset, col_count, 1)
        weight_own = weight_own + precise_dot(direction_all, alpha_own)
        if iteration + 1 < ITERS:
            resid_all = resid_all - precise_dot(image_all, alpha_coef)
            resid_now = lax.dynamic_slice_in_dim(resid_all, col_offset, col_count, 1)
            gram_new = full_gram(precise_dot(resid_all.T, resid_now)[None])[0]
            beta_coef = spd_solve(gram_rr, gram_new)
            direction_all = resid_all + precise_dot(direction_all, beta_coef)
            gram_rr = gram_new
    return weight_own


def solution(mesh):
    placed = (P("samp", None), P(), P(), P("samp", "tgt"))
    return jax.shard_map(
        body, mesh=mesh, in_specs=placed, out_specs=P("samp", "tgt"), check_vma=False
    )
```

profile of v0, /device:TPU:0, one launch (start us, length us, event | category | flops | bytes accessed | tf_op | source)
XLA Modules:
  0.0 1215.1 jit_solution(10789328759363507932)
XLA Ops:
  6.5 2.6 all_gather.24
  10.7 2.3 fusion.20
  22.8 50.4 %all-gather.7.cloned.1.call-done = bf16[4096,256]{1,0:T(8,128)(2,1)} async-done(((bf16[256,256]{1,0:T(8,128)(2,1)}), bf16[4096,256]{1,0:T(8,128)(2,1)}) %all-gather.7.cloned.1.call-update) | async-done | bytes 2097168 | tf_op jit(solution)/shard_map/all_gather | solution.py:57
  73.3 9.8 while.62
  83.1 2.2 broadcast.164.clone
  85.3 8.6 while.60
  96.3 91.8 %reduce-scatter.3.cloned.1.call-done = f32[256,256]{1,0:T(8,128)} async-done(((f32[4096,256]{1,0:T(8,128)}), f32[256,256]{1,0:T(8,128)}) %reduce-scatter.3.cloned.1.call-update) | async-done | bytes 262160 | tf_op jit(solution)/shard_map/reduce_scatter | solution.py:82
  190.6 114.9 %all-reduce.10.cloned.1.call-done = (f32[1,512,256]{1,2,0:T(8,128)}, f32[1,512,256]{1,2,0:T(8,128)}) async-done(((f32[1,512,256]{1,2,0:T(8,128)}, f32[1,512,256]{1,2,0:T(8,128)}), (f32[1,512,256]{1,2,0:T(8,128)}, f32[1,512,256]{1,2,0:T(8,128)})) %all-reduce.10.cloned.1.call-update) | async-done | bytes 1048592 | tf_op jit(solution)/shard_map/psum | solution.py:28
  305.5 2.3 all_gather.28
  307.9 7.1 all-gather.9.cloned.1.call-done
  315.0 2.6 copy.5
  320.1 11.7 cholesky.374
  332.0 9.8 custom-call.35
  344.3 11.7 cholesky.393
  356.1 10.0 custom-call.36
  367.6 11.7 cholesky.414
  380.0 9.8 custom-call.37
  391.3 11.7 cholesky.431
  408.6 12.0 while.64
  409.3 2.3 bitcast_dynamic-update-slice_fusion.6
  412.3 2.3 bitcast_dynamic-update-slice_fusion.6
  415.3 2.3 bitcast_dynamic-update-slice_fusion.6
  418.3 2.3 bitcast_dynamic-update-slice_fusion.6
  420.6 39.3 %custom-call.38 = f32[4,128,128]{1,2,0:T(8,128)S(1)} custom-call(f32[4,128,128]{2,1,0:T(8,128)S(1)} %get-tuple-element.377), custom_call_target="InvertDiagBlocksLowerTriangular" | custom-call | tf_op jit(solution)/shard_map/jit(_cho_solve)/triangular_solve | solution.py:17
  460.0 2.7 copy.7
  475.0 11.7 cholesky.446
  487.5 10.8 custom-call.39
  502.1 12.5 %cholesky.465 = f32[128,128]{1,0:T(8,128)S(1)} custom-call(f32[128,128]{1,0:T(8,128)} %cholesky.603), custom_call_target="Cholesky" | custom-call | tf_op jit(solution)/shard_map/jit(cholesky)/cholesky | solution.py:16
  515.3 10.6 custom-call.40
  529.1 12.5 %cholesky.486 = f32[128,128]{1,0:T(8,128)} custom-call(f32[128,128]{1,0:T(8,128)S(1)} %cholesky.608), custom_call_target="Cholesky" | custom-call | tf_op jit(solution)/shard_map/jit(cholesky)/cholesky | solution.py:16
  543.1 10.4 custom-call.41
  555.9 12.3 %cholesky.503 = f32[128,128]{1,0:T(8,128)} custom-call(f32[128,128]{1,0:T(8,128)S(1)} %convolution_subtract_fusion.26), custom_call_target="Cholesky" | custom-call | tf_op jit(solution)/shard_map/jit(cholesky)/cholesky | solution.py:16
  568.2 2.3 convolution_subtract_fusion
  571.4 1.8 convolution_bitcast_fusion.2
  578.3 105.3 %all-reduce.6.cloned.1.call-done = f32[1,512,256]{2,1,0:T(8,128)} async-done(((f32[1,512,256]{2,1,0:T(8,128)}), f32[1,512,256]{2,1,0:T(8,128)}) %all-reduce.6.cloned.1.call-update) | async-done | bytes 524304 | tf_op jit(solution)/shard_map/psum | solution.py:28
  684.4 14.8 %while.65 = (s32[]{:T(128)}, f32[512,512]{1,0:T(8,128)}, s32[4,2]{0,1:T(2,128)S(1)}, f32[4,128,128]{2,1,0:T(8,128)}, s32[]{:T(128)}) while((s32[]{:T(128)}, f32[512,512]{1,0:T(8,128)}, s32[4,2]{0,1:T(2,128)S(1)}, f32[4,128,128]{2,1,0:T(8,128)}, s32[]{:T(128)}) %tuple.227), condition=%wide.while_cond.clone, body=%wide.while_body.clone.sunk | while | flops 2 | bytes 132705 | solution.py:17
  685.5 2.9 bitcast_dynamic-update-slice_fusion.7
  689.1 3.0 bitcast_dynamic-update-slice_fusion.7
  692.7 2.9 bitcast_dynamic-update-slice_fusion.7
  696.3 2.9 bitcast_dynamic-update-slice_fusion.7
  699.2 40.8 %custom-call.42 = f32[4,128,128]{1,2,0:T(8,128)} custom-call(f32[4,128,128]{2,1,0:T(8,128)} %get-tuple-element.378), custom_call_target="InvertDiagBlocksLowerTriangular" | custom-call | tf_op jit(solution)/shard_map/jit(_cho_solve)/triangular_solve | solution.py:17
  752.9 59.5 %all-gather.15.cloned.1.call-done = bf16[4096,256]{1,0:T(8,128)(2,1)} async-done(((bf16[256,256]{1,0:T(8,128)(2,1)}), bf16[4096,256]{1,0:T(8,128)(2,1)}) %all-gather.15.cloned.1.call-update) | async-done | bytes 2097168 | tf_op jit(solution)/shard_map/all_gather | solution.py:57
  812.4 9.8 while.63
  822.2 2.2 broadcast.164
  824.4 8.6 while.61
  833.1 94.1 %reduce-scatter.5.cloned.1.call-done = f32[256,256]{1,0:T(8,128)} async-done(((f32[4096,256]{1,0:T(8,128)}), f32[256,256]{1,0:T(8,128)}) %reduce-scatter.5.cloned.1.call-update) | async-done | bytes 262160 | tf_op jit(solution)/shard_map/reduce_scatter | solution.py:82
  927.2 2.4 convolution_bitcast_fusion
  929.9 111.0 %all-reduce.8.cloned.1.call-done = f32[1,512,256]{1,2,0:T(8,128)} async-done(((f32[1,512,256]{1,2,0:T(8,128)}), f32[1,512,256]{1,2,0:T(8,128)}) %all-reduce.8.cloned.1.call-update) | async-done | bytes 524304 | tf_op jit(solution)/shard_map/psum | solution.py:28
  1042.0 8.5 all-gather.17.cloned.1.call-done
  1050.5 2.6 copy.10
  1055.6 11.7 cholesky.518
  1067.5 9.8 custom-call.43
  1079.8 11.7 cholesky.537
  1092.9 10.0 custom-call.44
  1104.4 11.7 cholesky.558
  1116.8 9.8 custom-call.45
  1128.1 11.7 cholesky.575
  1144.4 11.5 while.66
  1145.0 2.3 bitcast_dynamic-update-slice_fusion.8
  1147.9 2.3 bitcast_dynamic-update-slice_fusion.8
  1150.8 2.3 bitcast_dynamic-update-slice_fusion.8
  1153.7 2.2 bitcast_dynamic-update-slice_fusion.8
  1155.9 39.3 %custom-call.46 = f32[4,128,128]{1,2,0:T(8,128)S(1)} custom-call(f32[4,128,128]{2,1,0:T(8,128)S(1)} %get-tuple-element.379), custom_call_target="InvertDiagBlocksLowerTriangular" | custom-call | tf_op jit(solution)/shard_map/jit(_cho_solve)/triangular_solve | solution.py:17
  1200.2 1.6 convolution_subtract_fusion.14
  (260 shorter events, 138.2 us)
Async XLA Ops:
  6.5 4.2 copy-start
  6.5 6.5 copy-start.26
  6.5 66.7 %all-gather.7.cloned.1.call-start = ((), (), s32[]{:S(2)}) async-start(), calls=%async_computation.2 | async-start | bytes 2228224 | tf_op jit(solution)/shard_map/all_gather | solution.py:57
  9.9 178.2 %reduce-scatter.3.cloned.1.call-start = ((), (), s32[]{:S(2)}) async-start(), calls=%async_computation.3 | async-start | bytes 4456448 | tf_op jit(solution)/shard_map/reduce_scatter | solution.py:82
  93.9 0.9 copy-start.19
  93.9 211.5 %all-reduce.10.cloned.1.call-start = ((), (), s32[]{:S(2)}) async-start(), calls=%async_computation.12 | async-start | bytes 2097152 | tf_op jit(solution)/shard_map/psum | solution.py:28
  190.5 124.4 %all-gather.9.cloned.1.call-start = ((), (), s32[]{:S(2)}) async-start(), calls=%async_computation.4 | async-start | bytes 1572864 | tf_op jit(solution)/shard_map/all_gather | solution.py:29
  305.5 154.5 %all-gather.11.cloned.1.call-start = ((), (), s32[]{:S(2)}) async-start(), calls=%async_computation.5 | async-start | bytes 1572864 | tf_op jit(solution)/shard_map/all_gather | solution.py:29
  307.8 375.8 %all-reduce.6.cloned.1.call-start = ((), (), s32[]{:S(2)}) async-start(), calls=%async_computation.6 | async-start | bytes 1048576 | tf_op jit(solution)/shard_map/psum | solution.py:28
  315.0 2.7 copy-start.9
  319.1 1.0 copy-start.15
  459.9 7.9 copy-start.20
  460.0 2.7 copy-start.1
  462.6 2.3 copy-start.7
  468.2 3.4 copy-start.21
  471.2 1.6 copy-start.2
  471.7 2.2 copy-start.10
  472.0 2.0 copy-start.12
  474.1 1.0 copy-start.16
  500.8 0.7 copy-start.23
  528.4 0.7 copy-start.24
  568.2 7.6 copy-start.25
  570.6 0.8 copy-start.4
  573.2 166.8 %all-gather.13.cloned.1.call-start = ((), (), s32[]{:S(2)}) async-start(), calls=%async_computation.7 | async-start | bytes 1572864 | tf_op jit(solution)/shard_map/all_gather | solution.py:29
  683.6 128.7 %all-gather.15.cloned.1.call-start = ((), (), s32[]{:S(2)}) async-start(), calls=%async_computation.8 | async-start | bytes 2228224 | tf_op jit(solution)/shard_map/all_gather | solution.py:57
  699.2 44.9 %copy-start.6 = (f32[512,512]{1,0:T(8,128)S(1)}, f32[512,512]{1,0:T(8,128)}, u32[]{:S(2)}) copy-start(f32[512,512]{1,0:T(8,128)} %get-tuple-element.842) | copy-start | bytes 3145732
  740.0 5.5 copy-start.22
  749.6 1.4 copy-start.5
  752.8 174.4 %reduce-scatter.5.cloned.1.call-start = ((), (), s32[]{:S(2)}) async-start(), calls=%async_computation.9 | async-start | bytes 4456448 | tf_op jit(solution)/shard_map/reduce_scatter | solution.py:82
  833.0 207.9 %copy-start.3 = (f32[128,512]{1,0:T(8,128)S(1)}, f32[128,512]{1,0:T(8,128)}, u32[]{:S(2)}) copy-start(f32[128,512]{1,0:T(8,128)} %copy-done.2) | copy-start | bytes 786436
  833.0 207.9 %copy-start.13 = (f32[128,512]{1,0:T(8,128)S(1)}, f32[128,512]{1,0:T(8,128)}, u32[]{:S(2)}) copy-start(f32[128,512]{1,0:T(8,128)} %copy-done.12) | copy-start | bytes 786436
  833.0 207.9 %copy-start.18 = (f32[128,512]{1,0:T(8,128)S(1)}, f32[128,512]{1,0:T(8,128)}, u32[]{:S(2)}) copy-start(f32[128,512]{1,0:T(8,128)} %fusion.170) | copy-start | bytes 786436
  833.0 207.9 %all-reduce.8.cloned.1.call-start = ((), (), s32[]{:S(2)}) async-start(), calls=%async_computation.10 | async-start | bytes 1048576 | tf_op jit(solution)/shard_map/psum | solution.py:28
  929.7 120.8 %all-gather.17.cloned.1.call-start = ((), (), s32[]{:S(2)}) async-start(), calls=%async_computation.11 | async-start | bytes 1572864 | tf_op jit(solution)/shard_map/all_gather | solution.py:29
  1050.5 2.7 copy-start.11
  1054.6 1.0 copy-start.14
  1155.9 42.5 %copy-start.8 = (f32[512,512]{1,0:T(8,128)S(1)}, f32[512,512]{1,0:T(8,128)}, u32[]{:S(2)}) copy-start(f32[512,512]{1,0:T(8,128)} %get-tuple-element.844) | copy-start | bytes 3145732
  1204.9 1.4 copy-start.17
Sparse Core Ops, SparseCore 0:
  10.1 63.1 all-gather.6
  94.0 94.0 reduce-scatter.2
  193.4 111.9 all-reduce.9
  306.8 8.0 all-gather.8
  316.4 10.1 all-gather.10
  573.3 110.2 all-reduce.5
  685.2 8.0 all-gather.12
  752.9 59.3 all-gather.14
  833.1 94.0 reduce-scatter.4
  932.2 108.6 all-reduce.7
  1042.4 8.0 all-gather.16
where the time goes:
time: 1230 us; the launch traced here: 1220 us
  waiting for transfers between devices  643 us (52%)
  other arithmetic  372 us (30%)
  matrix products  111 us (9%)
  local copies, waits for them, and re-layouts  60.6 us (5%)
  between operations  22.3 us (2%)
    psum x3, waiting for transfers between devices, full_gram(): summed = lax.psum(stacked, 'samp')  331 us
    another operation x43, other arithmetic, spd_solve(): factor = jnp.linalg.cholesky(gram_matrix)  243 us
    reduce_scatter x2, waiting for transfers between devices, body(): lax.psum_scatter(lax.fori_loop(0, transpose_row_count // transpose_block_...  186 us
    another operation x8, other arithmetic, spd_solve(): return jax.scipy.linalg.cho_solve((factor, True), rhs_matrix)  124 us
    all_gather x2, waiting for transfers between devices, body(): lax.all_gather(direction_own.astype(jnp.bfloat16), 'samp', axis=0, tiled=...  110 us
    another operation x40, local copies, waits for them, and re-layouts, spd_solve(): return jax.scipy.linalg.cho_solve((factor, True), rhs_matrix)  38.5 us
    another operation x42, matrix products, spd_solve(): return jax.scipy.linalg.cho_solve((factor, True), rhs_matrix)  31.8 us
  transfers between devices with their start and end apart: 11, of which 9 were waited for; matrix products, arithmetic and copies ran while one was open for 18% of the time, Pallas kernels for 0%

commit v1 on v0

--- a/solution.py
+++ b/solution.py
@@ -25,7 +25,18 @@
 
 
 def full_gram(stacked):
-    summed = lax.psum(stacked, "samp")
+
+    def _wait_streams(chunk, along_axis):
+        local_part = chunk
+        axis_len = lax.psum(1, axis_name=along_axis)
+        for dev in [ii for ii in (1, 2, 4, 8, 16) if ii < axis_len]:
+            tile_out = lax.ppermute(
+                local_part, along_axis, perm=[(rr, rr ^ dev) for rr in range(axis_len)]
+            )
+            local_part = local_part + tile_out
+        return local_part
+
+    summed = _wait_streams(stacked, "samp")
     return lax.all_gather(summed, "tgt", axis=2, tiled=True)
 
 

time: 1230 us -> 1060 us (0.86)
  waiting for transfers between devices: 643 us -> 446 us
  starting transfers between devices: 0.93 us -> 22.5 us
  other arithmetic: 372 us -> 392 us
    psum x3 -> x0, waiting for transfers between devices: 331 us -> none  [full_gram(): summed = lax.psum(stacked, 'samp')]
    ppermute x0 -> x16, waiting for transfers between devices: none -> 170 us  [_wait_streams(): lax.ppermute(local_part, along_axis, perm=[(rr, rr ^ dev) for rr in range...]
    reduce_scatter x2, waiting for transfers between devices: 186 us -> 158 us  [body(): lax.psum_scatter(lax.fori_loop(0, transpose_row_count // transpose_block_...]
    ppermute x0 -> x16, starting transfers between devices: none -> 21.8 us  [_wait_streams(): lax.ppermute(local_part, along_axis, perm=[(rr, rr ^ dev) for rr in range...]
    add x0 -> x16, other arithmetic: none -> 13.7 us  [_wait_streams(): local_part = local_part + tile_out]
  transfers between devices with their start and end apart: 11 -> 24, of which waited for: 9 -> 17; matrix products, arithmetic and copies ran while one was open for 18% -> 16% of each run, Pallas kernels for 0% -> 0%
where the time goes in v1:
time: 1060 us; the launch traced here: 1050 us
  waiting for transfers between devices  446 us (42%)
  other arithmetic  392 us (37%)
  matrix products  103 us (10%)
  local copies, waits for them, and re-layouts  58.7 us (6%)
  between operations  23.9 us (2%)
  starting transfers between devices  22.5 us (2%)
    another operation x43, other arithmetic, spd_solve(): factor = jnp.linalg.cholesky(gram_matrix)  247 us
    ppermute x16, waiting for transfers between devices, _wait_streams(): lax.ppermute(local_part, along_axis, perm=[(rr, rr ^ dev) for rr in range...  170 us
    reduce_scatter x2, waiting for transfers between devices, body(): lax.psum_scatter(lax.fori_loop(0, transpose_row_count // transpose_block_...  158 us
    another operation x8, other arithmetic, spd_solve(): return jax.scipy.linalg.cho_solve((factor, True), rhs_matrix)  126 us
    all_gather x2, waiting for transfers between devices, body(): lax.all_gather(direction_own.astype(jnp.bfloat16), 'samp', axis=0, tiled=...  110 us
    another operation x40, local copies, waits for them, and re-layouts, spd_solve(): return jax.scipy.linalg.cho_solve((factor, True), rhs_matrix)  33.5 us
    another operation x42, matrix products, spd_solve(): return jax.scipy.linalg.cho_solve((factor, True), rhs_matrix)  27.5 us
    ppermute x16, starting transfers between devices, _wait_streams(): lax.ppermute(local_part, along_axis, perm=[(rr, rr ^ dev) for rr in range...  21.8 us
  transfers between devices with their start and end apart: 24, of which 17 were waited for; matrix products, arithmetic and copies ran while one was open for 16% of the time, Pallas kernels for 0%

profile of v1, /device:TPU:0, one launch (start us, length us, event | category | flops | bytes accessed | tf_op | source)
XLA Modules:
  0.0 1052.7 jit_solution(5057444541233907732)
XLA Ops:
  7.4 2.6 all_gather.24
  11.6 2.3 fusion.20
  23.6 50.4 %all-gather.7.cloned.1.call-done = bf16[4096,256]{1,0:T(8,128)(2,1)} async-done(((bf16[256,256]{1,0:T(8,128)(2,1)}), bf16[4096,256]{1,0:T(8,128)(2,1)}) %all-gather.7.cloned.1.call-update) | async-done | bytes 2097168 | tf_op jit(solution)/shard_map/all_gather | solution.py:68
  74.1 9.8 while.62
  83.9 2.2 broadcast.164.clone
  86.1 8.6 while.60
  97.7 32.0 %collective-permute-done.4 = f32[1,512,256]{1,2,0:T(8,128)S(1)} collective-permute-done((f32[1,512,256]{1,2,0:T(8,128)S(1)}, f32[1,512,256]{1,2,0:T(8,128)S(1)}, u32[]{:S(2)}, u32[]{:S(2)}) %collective-permute-start.4) | collective-permute-done | bytes 524320 | tf_op jit(solution)/shard_map/ppermute | solution.py:33
  130.8 63.8 %reduce-scatter.3.cloned.1.call-done = f32[256,256]{1,0:T(8,128)} async-done(((f32[4096,256]{1,0:T(8,128)}), f32[256,256]{1,0:T(8,128)}) %reduce-scatter.3.cloned.1.call-update) | async-done | bytes 262160 | tf_op jit(solution)/shard_map/reduce_scatter | solution.py:93
  198.7 3.4 collective-permute-start.6
  202.1 7.5 collective-permute-done
  214.2 8.7 collective-permute-done.1
  223.0 3.3 collective-permute-start.2
  226.3 12.7 %collective-permute-done.7 = f32[1,512,256]{1,2,0:T(8,128)S(1)} collective-permute-done((f32[1,512,256]{1,2,0:T(8,128)S(1)}, f32[1,512,256]{1,2,0:T(8,128)S(1)}, u32[]{:S(2)}, u32[]{:S(2)}) %collective-permute-start.7) | collective-permute-done | bytes 524320 | tf_op jit(solution)/shard_map/ppermute | solution.py:33
  240.0 7.2 collective-permute-done.2
  248.3 23.4 %collective-permute-done.3 = f32[1,512,256]{1,2,0:T(8,128)S(1)} collective-permute-done((f32[1,512,256]{1,2,0:T(8,128)S(1)}, f32[1,512,256]{1,2,0:T(8,128)S(1)}, u32[]{:S(2)}, u32[]{:S(2)}) %collective-permute-start.3) | collective-permute-done | bytes 524320 | tf_op jit(solution)/shard_map/ppermute | solution.py:33
  272.7 2.6 copy.7
  278.4 12.5 %cholesky.446 = f32[128,128]{1,0:T(8,128)S(1)} custom-call(f32[128,128]{1,0:T(8,128)} %cholesky.599), custom_call_target="Cholesky" | custom-call | tf_op jit(solution)/shard_map/jit(cholesky)/cholesky | solution.py:16
  291.6 11.3 %custom-call.39 = f32[1,128,128]{1,2,0:T(8,128)} custom-call(f32[1,128,128]{2,1,0:T(8,128)} %get-tuple-element.461), custom_call_target="InvertDiagBlocksLowerTriangular" | custom-call | tf_op jit(solution)/shard_map/jit(cholesky)/cholesky | solution.py:16
  304.0 2.5 all_gather.28
  306.5 2.5 copy.5
  311.8 11.7 %cholesky.374 = f32[128,128]{1,0:T(8,128)S(1)} custom-call(f32[128,128]{1,0:T(8,128)S(1)} %cholesky.586), custom_call_target="Cholesky" | custom-call | tf_op jit(solution)/shard_map/jit(cholesky)/cholesky | solution.py:16
  324.7 9.8 custom-call.35
  337.7 11.7 %cholesky.393 = f32[128,128]{1,0:T(8,128)S(1)} custom-call(f32[128,128]{1,0:T(8,128)S(1)} %cholesky.590), custom_call_target="Cholesky" | custom-call | tf_op jit(solution)/shard_map/jit(cholesky)/cholesky | solution.py:16
  350.0 10.2 custom-call.36
  362.7 11.7 %cholesky.414 = f32[128,128]{1,0:T(8,128)S(1)} custom-call(f32[128,128]{1,0:T(8,128)S(1)} %cholesky.595), custom_call_target="Cholesky" | custom-call | tf_op jit(solution)/shard_map/jit(cholesky)/cholesky | solution.py:16
  375.7 9.8 custom-call.37
  387.7 11.7 %cholesky.431 = f32[128,128]{1,0:T(8,128)S(1)} custom-call(f32[128,128]{1,0:T(8,128)S(1)} %convolution_subtract_fusion.24), custom_call_target="Cholesky" | custom-call | tf_op jit(solution)/shard_map/jit(cholesky)/cholesky | solution.py:16
  404.1 2.3 select_select_fusion.2
  406.5 11.5 %while.64 = (s32[]{:T(128)}, f32[512,512]{1,0:T(8,128)}, s32[4,2]{0,1:T(2,128)S(1)}, f32[4,128,128]{2,1,0:T(8,128)S(1)}, s32[]{:T(128)}) while((s32[]{:T(128)}, f32[512,512]{1,0:T(8,128)}, s32[4,2]{0,1:T(2,128)S(1)}, f32[4,128,128]{2,1,0:T(8,128)S(1)}, s32[]{:T(128)}) %tuple.186), condition=%wide.while_cond, body=%wide.while_body.sunk | while | flops 2 | bytes 131181 | solution.py:17
  407.1 2.3 bitcast_dynamic-update-slice_fusion.6
  410.0 2.3 bitcast_dynamic-update-slice_fusion.6
  412.9 2.3 bitcast_dynamic-update-slice_fusion.6
  418.7 40.1 %custom-call.38 = f32[4,128,128]{1,2,0:T(8,128)S(1)} custom-call(f32[4,128,128]{2,1,0:T(8,128)} %copy-done.28), custom_call_target="InvertDiagBlocksLowerTriangular" | custom-call | tf_op jit(solution)/shard_map/jit(_cho_solve)/triangular_solve | solution.py:17
  475.6 12.9 %cholesky.465 = f32[128,128]{1,0:T(8,128)S(1)} custom-call(f32[128,128]{1,0:T(8,128)} %cholesky.603), custom_call_target="Cholesky" | custom-call | tf_op jit(solution)/shard_map/jit(cholesky)/cholesky | solution.py:16
  489.1 10.6 %custom-call.40 = f32[1,128,128]{1,2,0:T(8,128)S(1)} custom-call(f32[1,128,128]{2,1,0:T(8,128)} %get-tuple-element.458), custom_call_target="InvertDiagBlocksLowerTriangular" | custom-call | tf_op jit(solution)/shard_map/jit(cholesky)/cholesky | solution.py:16
  505.1 12.5 %cholesky.486 = f32[128,128]{1,0:T(8,128)S(1)} custom-call(f32[128,128]{1,0:T(8,128)} %cholesky.608), custom_call_target="Cholesky" | custom-call | tf_op jit(solution)/shard_map/jit(cholesky)/cholesky | solution.py:16
  518.3 10.6 %custom-call.41 = f32[1,128,128]{1,2,0:T(8,128)S(1)} custom-call(f32[1,128,128]{2,1,0:T(8,128)} %get-tuple-element.455), custom_call_target="InvertDiagBlocksLowerTriangular" | custom-call | tf_op jit(solution)/shard_map/jit(cholesky)/cholesky | solution.py:16
  532.5 12.5 %cholesky.503 = f32[128,128]{1,0:T(8,128)} custom-call(f32[128,128]{1,0:T(8,128)S(1)} %convolution_subtract_fusion.23), custom_call_target="Cholesky" | custom-call | tf_op jit(solution)/shard_map/jit(cholesky)/cholesky | solution.py:16
  554.7 21.5 %collective-permute-done.11 = f32[1,512,256]{2,1,0:T(8,128)} collective-permute-done((f32[1,512,256]{2,1,0:T(8,128)}, f32[1,512,256]{2,1,0:T(8,128)}, u32[]{:S(2)}, u32[]{:S(2)}) %collective-permute-start.11) | collective-permute-done | bytes 524320 | tf_op jit(solution)/shard_map/ppermute | solution.py:33
  579.0 10.0 while.65
  589.0 40.7 %custom-call.42 = f32[4,128,128]{1,2,0:T(8,128)} custom-call(f32[4,128,128]{2,1,0:T(8,128)} %get-tuple-element.378), custom_call_target="InvertDiagBlocksLowerTriangular" | custom-call | tf_op jit(solution)/shard_map/jit(_cho_solve)/triangular_solve | solution.py:17
  640.7 59.1 %all-gather.15.cloned.1.call-done = bf16[4096,256]{1,0:T(8,128)(2,1)} async-done(((bf16[256,256]{1,0:T(8,128)(2,1)}), bf16[4096,256]{1,0:T(8,128)(2,1)}) %all-gather.15.cloned.1.call-update) | async-done | bytes 2097168 | tf_op jit(solution)/shard_map/all_gather | solution.py:68
  699.8 9.8 while.63
  711.8 8.6 while.61
  720.7 93.9 %reduce-scatter.5.cloned.1.call-done = f32[256,256]{1,0:T(8,128)} async-done(((f32[4096,256]{1,0:T(8,128)}), f32[256,256]{1,0:T(8,128)}) %reduce-scatter.5.cloned.1.call-update) | async-done | bytes 262160 | tf_op jit(solution)/shard_map/reduce_scatter | solution.py:93
  816.3 12.8 %collective-permute-done.12 = f32[1,512,256]{1,2,0:T(8,128)S(1)} collective-permute-done((f32[1,512,256]{1,2,0:T(8,128)S(1)}, f32[1,512,256]{1,2,0:T(8,128)S(1)}, u32[]{:S(2)}, u32[]{:S(2)}) %collective-permute-start.12) | collective-permute-done | bytes 524320 | tf_op jit(solution)/shard_map/ppermute | solution.py:33
  829.3 11.9 %collective-permute-done.13 = f32[1,512,256]{1,2,0:T(8,128)S(1)} collective-permute-done((f32[1,512,256]{1,2,0:T(8,128)S(1)}, f32[1,512,256]{1,2,0:T(8,128)S(1)}, u32[]{:S(2)}, u32[]{:S(2)}) %collective-permute-start.13) | collective-permute-done | bytes 524320 | tf_op jit(solution)/shard_map/ppermute | solution.py:33
  843.2 10.0 collective-permute-done.14
  853.3 3.3 collective-permute-start.15
  856.6 20.1 %collective-permute-done.15 = f32[1,512,256]{1,2,0:T(8,128)S(1)} collective-permute-done((f32[1,512,256]{1,2,0:T(8,128)S(1)}, f32[1,512,256]{1,2,0:T(8,128)S(1)}, u32[]{:S(2)}, u32[]{:S(2)}) %collective-permute-start.15) | collective-permute-done | bytes 524320 | tf_op jit(solution)/shard_map/ppermute | solution.py:33
  878.7 8.8 all-gather.17.cloned.1.call-done
  887.4 2.6 copy.10
  892.5 11.7 %cholesky.518 = f32[128,128]{1,0:T(8,128)S(1)} custom-call(f32[128,128]{1,0:T(8,128)S(1)} %cholesky.612), custom_call_target="Cholesky" | custom-call | tf_op jit(solution)/shard_map/jit(cholesky)/cholesky | solution.py:16
  904.4 9.8 custom-call.43
  916.7 12.1 %cholesky.537 = f32[128,128]{1,0:T(8,128)S(1)} custom-call(f32[128,128]{1,0:T(8,128)S(1)} %cholesky.616), custom_call_target="Cholesky" | custom-call | tf_op jit(solution)/shard_map/jit(cholesky)/cholesky | solution.py:16
  930.1 9.8 custom-call.44
  941.5 11.7 %cholesky.558 = f32[128,128]{1,0:T(8,128)S(1)} custom-call(f32[128,128]{1,0:T(8,128)S(1)} %cholesky.621), custom_call_target="Cholesky" | custom-call | tf_op jit(solution)/shard_map/jit(cholesky)/cholesky | solution.py:16
  954.0 9.8 custom-call.45
  965.2 11.9 %cholesky.575 = f32[128,128]{1,0:T(8,128)S(1)} custom-call(f32[128,128]{1,0:T(8,128)S(1)} %convolution_subtract_fusion.22), custom_call_target="Cholesky" | custom-call | tf_op jit(solution)/shard_map/jit(cholesky)/cholesky | solution.py:16
  981.4 11.5 %while.66 = (s32[]{:T(128)}, f32[512,512]{1,0:T(8,128)}, s32[4,2]{0,1:T(2,128)S(1)}, f32[4,128,128]{2,1,0:T(8,128)S(1)}, s32[]{:T(128)}) while((s32[]{:T(128)}, f32[512,512]{1,0:T(8,128)}, s32[4,2]{0,1:T(2,128)S(1)}, f32[4,128,128]{2,1,0:T(8,128)S(1)}, s32[]{:T(128)}) %tuple.222), condition=%wide.while_cond.clone.1, body=%wide.while_body.clone.1.sunk | while | flops 2 | bytes 131181 | solution.py:17
  982.0 2.3 bitcast_dynamic-update-slice_fusion.8
  984.9 2.3 bitcast_dynamic-update-slice_fusion.8
  987.8 2.3 bitcast_dynamic-update-slice_fusion.8
  992.9 39.3 %custom-call.46 = f32[4,128,128]{1,2,0:T(8,128)S(1)} custom-call(f32[4,128,128]{2,1,0:T(8,128)S(1)} %get-tuple-element.379), custom_call_target="InvertDiagBlocksLowerTriangular" | custom-call | tf_op jit(solution)/shard_map/jit(_cho_solve)/triangular_solve | solution.py:17
  (309 shorter events, 184.4 us)
Async XLA Ops:
  7.4 4.2 copy-start
  7.4 6.5 copy-start.31
  7.4 66.7 %all-gather.7.cloned.1.call-start = ((), (), s32[]{:S(2)}) async-start(), calls=%async_computation.2 | async-start | bytes 2228224 | tf_op jit(solution)/shard_map/all_gather | solution.py:68
  10.7 183.9 %reduce-scatter.3.cloned.1.call-start = ((), (), s32[]{:S(2)}) async-start(), calls=%async_computation.3 | async-start | bytes 4456448 | tf_op jit(solution)/shard_map/reduce_scatter | solution.py:93
  94.7 0.9 copy-start.22
  94.8 177.9 %all-gather.11.cloned.1.call-start = ((), (), s32[]{:S(2)}) async-start(), calls=%async_computation.5 | async-start | bytes 1572864 | tf_op jit(solution)/shard_map/all_gather | solution.py:40
  96.3 33.3 %collective-permute-start.4 = (f32[1,512,256]{1,2,0:T(8,128)S(1)}, f32[1,512,256]{1,2,0:T(8,128)S(1)}, u32[]{:S(2)}, u32[]{:S(2)}) collective-permute-start(f32[1,512,256]{1,2,0:T(8,128)S(1)} %convolution_bitcast_fusion.3), channel_id=1, source_target_pairs={{0,2},{2,0},{4,6},{6,4},{8,10},{10,8},{12,14},{14,12},{16,18},{18,... | collective-permute-start | bytes 1572872 | tf_op jit(solution)/shard_map/ppermute | solution.py:33
  129.7 67.8 %collective-permute-start.5 = (f32[1,512,256]{1,2,0:T(8,128)S(1)}, f32[1,512,256]{1,2,0:T(8,128)}, u32[]{:S(2)}, u32[]{:S(2)}) collective-permute-start(f32[1,512,256]{1,2,0:T(8,128)S(1)} %add.301), channel_id=1, source_target_pairs={{0,4},{2,6},{4,0},{6,2},{8,12},{10,14},{12,8},{14,10},{16,20},{18,... | collective-permute-start | bytes 1572872 | tf_op jit(solution)/shard_map/ppermute | solution.py:33
  196.2 13.4 %collective-permute-start = (f32[1,512,256]{1,2,0:T(8,128)S(1)}, f32[1,512,256]{1,2,0:T(8,128)S(1)}, u32[]{:S(2)}, u32[]{:S(2)}) collective-permute-start(f32[1,512,256]{1,2,0:T(8,128)S(1)} %convolution_bitcast_fusion.4), channel_id=1, source_target_pairs={{0,2},{2,0},{4,6},{6,4},{8,10},{10,8},{12,14},{14,12},{16,18},{18,... | collective-permute-start | bytes 1572872 | tf_op jit(solution)/shard_map/ppermute | solution.py:33
  198.7 15.1 %collective-permute-start.6 = (f32[1,512,256]{1,2,0:T(8,128)S(1)}, f32[1,512,256]{1,2,0:T(8,128)S(1)}, u32[]{:S(2)}, u32[]{:S(2)}) collective-permute-start(f32[1,512,256]{1,2,0:T(8,128)S(1)} %add.302), channel_id=1, source_target_pairs={{0,8},{2,10},{4,12},{6,14},{8,0},{10,2},{12,4},{14,6},{16,24},{18,... | collective-permute-start | bytes 1572872 | tf_op jit(solution)/shard_map/ppermute | solution.py:33
  209.7 13.2 %collective-permute-start.1 = (f32[1,512,256]{1,2,0:T(8,128)S(1)}, f32[1,512,256]{1,2,0:T(8,128)S(1)}, u32[]{:S(2)}, u32[]{:S(2)}) collective-permute-start(f32[1,512,256]{1,2,0:T(8,128)S(1)} %add.297), channel_id=1, source_target_pairs={{0,4},{2,6},{4,0},{6,2},{8,12},{10,14},{12,8},{14,10},{16,20},{18,... | collective-permute-start | bytes 1572872 | tf_op jit(solution)/shard_map/ppermute | solution.py:33
  213.9 25.1 %collective-permute-start.7 = (f32[1,512,256]{1,2,0:T(8,128)S(1)}, f32[1,512,256]{1,2,0:T(8,128)S(1)}, u32[]{:S(2)}, u32[]{:S(2)}) collective-permute-start(f32[1,512,256]{1,2,0:T(8,128)S(1)} %add.303), channel_id=1, source_target_pairs={{0,16},{2,18},{4,20},{6,22},{8,24},{10,26},{12,28},{14,30},{16,0},... | collective-permute-start | bytes 1572872 | tf_op jit(solution)/shard_map/ppermute | solution.py:33
  223.0 24.2 %collective-permute-start.2 = (f32[1,512,256]{1,2,0:T(8,128)S(1)}, f32[1,512,256]{1,2,0:T(8,128)}, u32[]{:S(2)}, u32[]{:S(2)}) collective-permute-start(f32[1,512,256]{1,2,0:T(8,128)S(1)} %add.298), channel_id=1, source_target_pairs={{0,8},{2,10},{4,12},{6,14},{8,0},{10,2},{12,4},{14,6},{16,24},{18,... | collective-permute-start | bytes 1572872 | tf_op jit(solution)/shard_map/ppermute | solution.py:33
  239.9 66.6 %all-gather.9.cloned.1.call-start = ((), (), s32[]{:S(2)}) async-start(), calls=%async_computation.4 | async-start | bytes 1572864 | tf_op jit(solution)/shard_map/all_gather | solution.py:40
  248.3 23.4 %collective-permute-start.3 = (f32[1,512,256]{1,2,0:T(8,128)S(1)}, f32[1,512,256]{1,2,0:T(8,128)S(1)}, u32[]{:S(2)}, u32[]{:S(2)}) collective-permute-start(f32[1,512,256]{1,2,0:T(8,128)S(1)} %add.299), channel_id=1, source_target_pairs={{0,16},{2,18},{4,20},{6,22},{8,24},{10,26},{12,28},{14,30},{16,0},... | collective-permute-start | bytes 1572872 | tf_op jit(solution)/shard_map/ppermute | solution.py:33
  272.6 357.1 %all-gather.13.cloned.1.call-start = ((), (), s32[]{:S(2)}) async-start(), calls=%async_computation.6 | async-start | bytes 1572864 | tf_op jit(solution)/shard_map/all_gather | solution.py:40
  272.7 2.6 copy-start.2
  276.8 1.0 copy-start.15
  310.8 1.0 copy-start.17
  418.0 0.7 copy-start.28
  458.8 2.3 copy-start.8
  465.7 1.9 copy-start.4
  466.1 1.5 copy-start.21
  466.5 2.2 copy-start.13
  467.6 2.9 copy-start.19
  467.6 4.1 copy-start.3
  467.6 4.1 copy-start.29
  468.7 4.3 copy-start.6
  470.5 29.3 %collective-permute-start.8 = (f32[1,512,256]{2,1,0:T(8,128)}, f32[1,512,256]{2,1,0:T(8,128)}, u32[]{:S(2)}, u32[]{:S(2)}) collective-permute-start(f32[1,512,256]{2,1,0:T(8,128)} %convolution_bitcast_fusion.2), channel_id=1, source_target_pairs={{0,2},{2,0},{4,6},{6,4},{8,10},{10,8},{12,14},{14,12},{16,18},{18,... | collective-permute-start | bytes 1572872 | tf_op jit(solution)/shard_map/ppermute | solution.py:33
  474.2 0.7 copy-start.24
  499.8 2.4 copy-start.25
  501.9 27.0 %collective-permute-start.9 = (f32[1,512,256]{2,1,0:T(8,128)}, f32[1,512,256]{2,1,0:T(8,128)}, u32[]{:S(2)}, u32[]{:S(2)}) collective-permute-start(f32[1,512,256]{2,1,0:T(8,128)} %add.305), channel_id=1, source_target_pairs={{0,4},{2,6},{4,0},{6,2},{8,12},{10,14},{12,8},{14,10},{16,20},{18,... | collective-permute-start | bytes 1572872 | tf_op jit(solution)/shard_map/ppermute | solution.py:33
  503.8 0.7 copy-start.26
  528.9 2.1 copy-start.27
  531.0 16.9 %collective-permute-start.10 = (f32[1,512,256]{2,1,0:T(8,128)}, f32[1,512,256]{2,1,0:T(8,128)}, u32[]{:S(2)}, u32[]{:S(2)}) collective-permute-start(f32[1,512,256]{2,1,0:T(8,128)} %add.306), channel_id=1, source_target_pairs={{0,8},{2,10},{4,12},{6,14},{8,0},{10,2},{12,4},{14,6},{16,24},{18,... | collective-permute-start | bytes 1572872 | tf_op jit(solution)/shard_map/ppermute | solution.py:33
  545.0 7.3 copy-start.30
  550.0 26.1 %collective-permute-start.11 = (f32[1,512,256]{2,1,0:T(8,128)}, f32[1,512,256]{2,1,0:T(8,128)}, u32[]{:S(2)}, u32[]{:S(2)}) collective-permute-start(f32[1,512,256]{2,1,0:T(8,128)} %add.307), channel_id=1, source_target_pairs={{0,16},{2,18},{4,20},{6,22},{8,24},{10,26},{12,28},{14,30},{16,0},... | collective-permute-start | bytes 1572872 | tf_op jit(solution)/shard_map/ppermute | solution.py:33
  554.7 24.3 %copy-start.9 = (f32[512,512]{1,0:T(8,128)S(1)}, f32[512,512]{1,0:T(8,128)}, u32[]{:S(2)}) copy-start(f32[512,512]{1,0:T(8,128)} %select_select_fusion.1) | copy-start | bytes 3145732
  578.2 121.5 %all-gather.15.cloned.1.call-start = ((), (), s32[]{:S(2)}) async-start(), calls=%async_computation.7 | async-start | bytes 2228224 | tf_op jit(solution)/shard_map/all_gather | solution.py:68
  629.7 4.1 copy-start.12
  629.7 4.5 copy-start.23
  637.4 1.4 copy-start.7
  640.6 174.0 %reduce-scatter.5.cloned.1.call-start = ((), (), s32[]{:S(2)}) async-start(), calls=%async_computation.8 | async-start | bytes 4456448 | tf_op jit(solution)/shard_map/reduce_scatter | solution.py:93
  720.4 167.0 %all-gather.17.cloned.1.call-start = ((), (), s32[]{:S(2)}) async-start(), calls=%async_computation.9 | async-start | bytes 1572864 | tf_op jit(solution)/shard_map/all_gather | solution.py:40
  816.3 12.9 %collective-permute-start.12 = (f32[1,512,256]{1,2,0:T(8,128)S(1)}, f32[1,512,256]{1,2,0:T(8,128)S(1)}, u32[]{:S(2)}, u32[]{:S(2)}) collective-permute-start(f32[1,512,256]{1,2,0:T(8,128)S(1)} %convolution_bitcast_fusion), channel_id=1, source_target_pairs={{0,2},{2,0},{4,6},{6,4},{8,10},{10,8},{12,14},{14,12},{16,18},{18,... | collective-permute-start | bytes 1572872 | tf_op jit(solution)/shard_map/ppermute | solution.py:33
  829.2 12.0 %collective-permute-start.13 = (f32[1,512,256]{1,2,0:T(8,128)S(1)}, f32[1,512,256]{1,2,0:T(8,128)S(1)}, u32[]{:S(2)}, u32[]{:S(2)}) collective-permute-start(f32[1,512,256]{1,2,0:T(8,128)S(1)} %add.311), channel_id=1, source_target_pairs={{0,4},{2,6},{4,0},{6,2},{8,12},{10,14},{12,8},{14,10},{16,20},{18,... | collective-permute-start | bytes 1572872 | tf_op jit(solution)/shard_map/ppermute | solution.py:33
  841.3 36.2 %copy-start.5 = (f32[128,512]{1,0:T(8,128)S(1)}, f32[128,512]{1,0:T(8,128)}, u32[]{:S(2)}) copy-start(f32[128,512]{1,0:T(8,128)} %copy-done.4) | copy-start | bytes 786436
  841.3 36.2 %copy-start.14 = (f32[128,512]{1,0:T(8,128)S(1)}, f32[128,512]{1,0:T(8,128)}, u32[]{:S(2)}) copy-start(f32[128,512]{1,0:T(8,128)} %copy-done.13) | copy-start | bytes 786436
  841.4 36.2 %copy-start.20 = (f32[128,512]{1,0:T(8,128)S(1)}, f32[128,512]{1,0:T(8,128)}, u32[]{:S(2)}) copy-start(f32[128,512]{1,0:T(8,128)} %copy-done.19) | copy-start | bytes 786436
  841.4 11.8 %collective-permute-start.14 = (f32[1,512,256]{1,2,0:T(8,128)S(1)}, f32[1,512,256]{1,2,0:T(8,128)S(1)}, u32[]{:S(2)}, u32[]{:S(2)}) collective-permute-start(f32[1,512,256]{1,2,0:T(8,128)S(1)} %add.312), channel_id=1, source_target_pairs={{0,8},{2,10},{4,12},{6,14},{8,0},{10,2},{12,4},{14,6},{16,24},{18,... | collective-permute-start | bytes 1572872 | tf_op jit(solution)/shard_map/ppermute | solution.py:33
  853.3 23.4 %collective-permute-start.15 = (f32[1,512,256]{1,2,0:T(8,128)S(1)}, f32[1,512,256]{1,2,0:T(8,128)S(1)}, u32[]{:S(2)}, u32[]{:S(2)}) collective-permute-start(f32[1,512,256]{1,2,0:T(8,128)S(1)} %add.313), channel_id=1, source_target_pairs={{0,16},{2,18},{4,20},{6,22},{8,24},{10,26},{12,28},{14,30},{16,0},... | collective-permute-start | bytes 1572872 | tf_op jit(solution)/shard_map/ppermute | solution.py:33
  887.4 2.6 copy-start.11
  891.5 1.0 copy-start.16
  992.9 42.5 %copy-start.10 = (f32[512,512]{1,0:T(8,128)S(1)}, f32[512,512]{1,0:T(8,128)}, u32[]{:S(2)}) copy-start(f32[512,512]{1,0:T(8,128)} %get-tuple-element.836) | copy-start | bytes 3145732
  1041.9 1.4 copy-start.18
  1041.9 3.3 copy-start.1
Sparse Core Ops, SparseCore 0:
  10.9 63.1 all-gather.6
  94.9 99.6 reduce-scatter.2
  640.8 58.9 all-gather.14
  720.5 94.0 reduce-scatter.4
Sparse Core Ops, SparseCore 1:
  240.0 6.2 all-gather.10
  272.7 7.2 all-gather.8
  578.3 7.5 all-gather.12
  877.6 9.7 all-gather.16
